TPU v7x, 32 devices: a whole 2x2x4 slice. The times are simulated.
32 devices in a mesh: dp: 16 (over z, x, core), emb: 2 (over y).
Axes of the slice: x: 2, y: 2, z: 4, core: 2. Of those that a mesh axis runs over, the one named last changes fastest.
Arguments:
- cur_ids: int32 [8192], P(('dp', 'emb')), may hold values from 0 to 3071, as said below
- prev_ids: int32 [8192], P(('dp', 'emb')), may hold values from 0 to 3071, as said below
- prev_grads: bfloat16 [8192, 128], P(('dp', 'emb')), may hold values from -6 to 6
- row_place: int32 [3072], replicated, may hold values from 0 to 3071, as said below
- table: float32 [3072, 128], P('emb'), may hold values from -6 to 6
- accum: float32 [3072, 128], P('emb'), may hold values from 0.05 to 2
- labels: float32 [8192], P('dp'), may hold values from 0 to 1
- gain: float32 [128], replicated, may hold values from 0.5 to 1.5
- w_gate: bfloat16 [128, 4096], P(None, 'emb'), may hold values from -0.5 to 0.5
- w_up: bfloat16 [128, 4096], P(None, 'emb'), may hold values from -0.5 to 0.5
- w_out: bfloat16 [4096], P('emb'), may hold values from -0.09375 to 0.09375
Outputs:
- new_table: float32 [3072, 128], P('emb')
- new_accum: float32 [3072, 128], P('emb')
- grad_gate: float32 [128, 4096], P(None, 'emb')
- grad_up: float32 [128, 4096], P(None, 'emb')
- emb_grad: float32 [8192, 128], P(('dp', 'emb'))
Inputs may be any that keep to these rules, and one draw needn't show every extreme that they name: A permutation of the table rows; row i is stored on shard row_place[i] // 1536 of emb at position row_place[i] % 1536. `cur_ids`: the 256 ids of one device name rows of one shard at most 256 times, and exactly 256 times for some shard. `prev_ids`: the 256 ids of one device name rows of one shard at most 256 times, and exactly 256 times for some shard.
All inputs are finite; a program needn't handle non-finite values.
Results may differ from a plain program's by a relative error of at most 0.0069.
Values may be sent and summed in bfloat16 or wider, within the bound.
A program may use at most 64 MiB of HBM per device.

v0:
```python
import math

import jax
import jax.numpy as jnp
from jax import lax
from jax.sharding import PartitionSpec as P

loss_weight = 64.0
learn_rate = 0.1
norm_eps = 1e-06


def pack_slots(stored, rows_shard, capacity, shards):
    owner_shard = stored // rows_shard
    slot_index = stored % rows_shard
    matches = (owner_shard[:, None] == jnp.arange(shards, dtype=jnp.int32)[None, :]).astype(
        jnp.int32
    )
    ranking = jnp.sum(jnp.cumsum(matches, axis=0) * matches, axis=1) - 1
    return (slot_index, owner_shard * capacity + ranking)


def on_device(
    cur_ids, prev_ids, prev_grads, row_place, table, accum, labels, gain, w_gate, w_up, w_out
):
    shards = lax.axis_size("emb")
    replicas = lax.axis_size("dp")
    rows_shard = table.shape[0]
    emb_width = table.shape[1]
    tok_rows = cur_ids.shape[0]
    capacity = min(tok_rows, 2 * tok_rows // shards)
    slot_index, target_pos = pack_slots(row_place[cur_ids], rows_shard, capacity, shards)
    requests = (
        jnp.full((shards * capacity,), -1, jnp.int32)
        .at[target_pos]
        .set(slot_index)
        .reshape(shards, capacity)
    )
    wanted = lax.all_to_all(requests, "emb", split_axis=0, concat_axis=0, tiled=True)
    fetched = table[jnp.maximum(wanted, 0)]
    fetched = jnp.where((wanted >= 0)[..., None], fetched, 0.0).astype(jnp.bfloat16)
    answers = lax.all_to_all(fetched, "emb", split_axis=0, concat_axis=0, tiled=True)
    looked_up = answers.reshape(shards * capacity, emb_width)[target_pos]
    grad_slot, grad_pos = pack_slots(row_place[prev_ids], rows_shard, capacity, shards)
    slot_pack = (
        jnp.full((shards * capacity,), -1, jnp.int32)
        .at[grad_pos]
        .set(grad_slot)
        .reshape(shards, capacity)
    )
    grad_pack = jnp.zeros((shards * capacity, emb_width), jnp.bfloat16).at[grad_pos].set(prev_grads)
    grad_pack = grad_pack.reshape(shards, capacity, emb_width)
    got_rows, got_slots = (
        lax.all_to_all(grad_pack, "emb", split_axis=0, concat_axis=0, tiled=True),
        lax.all_to_all(slot_pack, "emb", split_axis=0, concat_axis=0, tiled=True),
    )
    one_hot = (jnp.arange(rows_shard, dtype=jnp.int32)[:, None] == got_slots.reshape(1, -1)).astype(
        jnp.bfloat16
    )
    table_grad = jnp.dot(
        one_hot, got_rows.reshape(-1, emb_width), preferred_element_type=jnp.float32
    )
    values = looked_up.astype(jnp.float32)
    inverse_rms = lax.rsqrt(jnp.mean(values * values, axis=1, keepdims=True) + norm_eps)
    normed = (values * inverse_rms * gain).astype(jnp.bfloat16)
    gathered = lax.all_gather(normed, "emb", axis=0, tiled=True)
    gate_proj = jnp.dot(gathered, w_gate, preferred_element_type=jnp.float32)
    up_proj = jnp.dot(gathered, w_up, preferred_element_type=jnp.float32)
    sigmoid_gate = jax.nn.sigmoid(gate_proj)
    activated = gate_proj * sigmoid_gate
    hidden = (activated * up_proj).astype(jnp.bfloat16)
    partial_value = jnp.dot(hidden, w_out, preferred_element_type=jnp.float32)
    logits = lax.psum(partial_value, "emb")
    slopes = loss_weight * (jax.nn.sigmoid(logits) - labels)
    back_hidden = slopes[:, None] * w_out.astype(jnp.float32)[None, :]
    back_gate = (
        back_hidden * up_proj * sigmoid_gate * (1.0 + gate_proj * (1.0 - sigmoid_gate))
    ).astype(jnp.bfloat16)
    back_up = (back_hidden * activated).astype(jnp.bfloat16)
    contract = (((0,), (0,)), ((), ()))
    gate_part = lax.dot_general(gathered, back_gate, contract, preferred_element_type=jnp.float32)
    up_part = lax.dot_general(gathered, back_up, contract, preferred_element_type=jnp.float32)
    across = (((1,), (1,)), ((), ()))
    result = lax.dot_general(back_gate, w_gate, across, preferred_element_type=jnp.float32)
    back_normed = lax.psum_scatter(
        result + lax.dot_general(back_up, w_up, across, preferred_element_type=jnp.float32),
        "emb",
        scatter_dimension=0,
        tiled=True,
    )
    scaled = back_normed * gain
    emb_grad = inverse_rms * scaled - values * inverse_rms**3 * jnp.mean(
        values * scaled, axis=1, keepdims=True
    )
    gate_sum, up_sum, total_grad = lax.psum((gate_part, up_part, table_grad), "dp")
    new_accum = accum + total_grad * total_grad
    new_table = table - learn_rate * total_grad * lax.rsqrt(new_accum)
    tower_scale = 1.0 / math.sqrt(tok_rows * shards * replicas)
    return (new_table, new_accum, gate_sum * tower_scale, up_sum * tower_scale, emb_grad)


def solution(mesh):
    placed = (
        P(("dp", "emb")),
        P(("dp", "emb")),
        P(("dp", "emb"), None),
        P(),
        P("emb", None),
        P("emb", None),
        P("dp"),
        P(),
        P(None, "emb"),
        P(None, "emb"),
        P("emb"),
    )
    return jax.shard_map(
        on_device,
        mesh=mesh,
        in_specs=placed,
        out_specs=(
            P("emb", None),
            P("emb", None),
            P(None, "emb"),
            P(None, "emb"),
            P(("dp", "emb"), None),
        ),
        check_vma=False,
    )
```

profile of v0, /device:TPU:1, one launch (start us, length us, event | category | flops | bytes accessed | tf_op | source)
XLA Modules:
  0.0 190.6 jit_solution(4421274131920714523)
XLA Ops:
  8.0 0.7 compare_select_fusion.3
  8.8 1.9 %gather_fusion.1 = s32[256]{0:T(256)S(1)} fusion(s32[3072]{0:T(1024)} %param.14, s32[1024]{0:T(1024)S(1)} %pad_clamp_fusion.2), kind=kCustom, calls=%fused_computation.1 | custom fusion | bytes 3072 | tf_op jit(solution)/shard_map/gather | solution.py:32
  10.8 0.6 reduce-window.16
  11.4 0.2 slice_reduce_fusion
  11.6 0.2 reduce-window.19
  11.8 0.1 add_bitcast_fusion
  11.9 2.0 %scatter_custom_fusion.2 = s32[512]{0:T(512)} fusion(s32[256]{0:T(256)S(1)} %bitcast.69, s32[256]{0:T(256)S(1)} %get-tuple-element.20, s32[]{:T(128)} %constant.51.clone.1), kind=kCustom, calls=%fused_computation.79 | custom fusion | bytes 2052 | tf_op jit(solution)/shard_map/scatter | solution.py:36
  13.9 3.3 %all-to-all-start.2 = ((s32[2,1,256]{2,1,0:T(1,128)}), s32[2,1,256]{2,1,0:T(1,128)S(1)}, u32[]{:S(2)}, u32[]{:S(2)}) async-start(s32[2,1,256]{2,1,0:T(1,128)} %bitcast.16), calls=%async_computation.2 | async-start | bytes 4096 | tf_op jit(solution)/shard_map/all_to_all | solution.py:39
  17.2 0.7 compare_select_fusion.5
  17.9 1.9 %gather_fusion = s32[256]{0:T(256)S(1)} fusion(s32[3072]{0:T(1024)} %param.14, s32[1024]{0:T(1024)S(1)} %pad_clamp_fusion.3), kind=kCustom, calls=%fused_computation | custom fusion | bytes 3072 | tf_op jit(solution)/shard_map/gather | solution.py:44
  19.9 0.6 reduce-window.14
  20.5 0.2 slice_reduce_fusion.1
  20.7 0.2 reduce-window.15
  20.9 0.1 add_bitcast_fusion.1
  21.0 0.7 reshape.317
  21.7 0.7 convert_element_type.38
  22.4 2.0 %scatter_custom_fusion = s32[512]{0:T(512)} fusion(s32[256]{0:T(256)S(1)} %bitcast.77, s32[256]{0:T(256)S(1)} %get-tuple-element.21, s32[]{:T(128)} %constant.51.clone.1), kind=kCustom, calls=%fused_computation.81 | custom fusion | bytes 2052 | tf_op jit(solution)/shard_map/scatter | solution.py:48
  24.4 2.1 %scatter_custom_fusion.1 = bf16[512,128]{1,0:T(8,128)(2,1)} fusion(s32[256]{0:T(256)S(1)} %bitcast.78, bf16[256,128]{1,0:T(8,128)(2,1)} %param.13, bf16[]{:T(256)} %constant.58.clone.1), kind=kCustom, calls=%fused_computation.36 | custom fusion | bytes 131584 | tf_op jit(solution)/shard_map/scatter | solution.py:51
  26.5 3.2 %all-to-all-start = ((s32[2,1,256]{2,1,0:T(1,128)}), s32[2,1,256]{2,1,0:T(1,128)S(1)}, u32[]{:S(2)}, u32[]{:S(2)}) async-start(s32[2,1,256]{2,1,0:T(1,128)} %bitcast.6), calls=%async_computation | async-start | bytes 4096 | tf_op jit(solution)/shard_map/all_to_all | solution.py:55
  29.7 2.2 %gather_fusion.2 = bf16[512,128]{1,0:T(8,128)(2,1)S(1)} fusion(f32[1536,128]{1,0:T(8,128)} %param.15, s32[1024]{0:T(1024)S(1)} %pad_clamp_fusion.1), kind=kCustom, calls=%fused_computation.2 | custom fusion | bytes 264192 | tf_op jit(solution)/shard_map/gather | solution.py:40
  31.9 0.9 all-to-all-done
  32.8 3.4 %all-to-all-start.1 = ((bf16[2,256,128]{2,1,0:T(8,128)(2,1)}), bf16[2,256,128]{2,1,0:T(8,128)(2,1)S(1)}, u32[]{:S(2)}, u32[]{:S(2)}) async-start(bf16[2,256,128]{2,1,0:T(8,128)(2,1)} %bitcast.8), calls=%async_computation.1 | async-start | bytes 262144 | tf_op jit(solution)/shard_map/all_to_all | solution.py:54
  36.2 0.8 select_convert_fusion
  37.0 2.5 %all-to-all-done.1 = bf16[2,256,128]{2,1,0:T(8,128)(2,1)S(1)} async-done(((bf16[2,256,128]{2,1,0:T(8,128)(2,1)}), bf16[2,256,128]{2,1,0:T(8,128)(2,1)S(1)}, u32[]{:S(2)}, u32[]{:S(2)}) %all-to-all-start.1) | async-done | bytes 131104 | tf_op jit(solution)/shard_map/all_to_all | solution.py:54
  39.5 3.4 %all-to-all-start.3 = ((bf16[2,256,128]{2,1,0:T(8,128)(2,1)}), bf16[2,256,128]{2,1,0:T(8,128)(2,1)S(1)}, u32[]{:S(2)}, u32[]{:S(2)}) async-start(bf16[2,256,128]{2,1,0:T(8,128)(2,1)} %select_convert_fusion), calls=%async_computation.3 | async-start | bytes 262144 | tf_op jit(solution)/shard_map/all_to_all | solution.py:42
  42.9 1.5 fusion.5
  44.4 1.8 all-to-all-done.3
  46.2 0.9 gather_fusion.3
  47.0 0.1 fusion.9
  47.2 0.1 fusion.11
  47.3 3.8 %all_gather.3 = bf16[512,128]{1,0:T(8,128)(2,1)S(1)} all-gather(bf16[256,128]{1,0:T(8,128)(2,1)S(1)} %fusion.11), channel_id=1, replica_groups=mesh['dp'=16,'emb'=2] {'emb'}, dimensions={0}, use_global_device_ids=true | all-gather | bytes 196608 | tf_op jit(solution)/shard_map/all_gather | solution.py:66
  51.1 0.7 fusion.29
  51.8 0.7 fusion.30
  52.5 1.2 fusion.6
  53.7 1.3 copy-done.3
  55.0 3.8 %psum.29 = f32[512]{0:T(512)S(1)} all-reduce(f32[512]{0:T(512)S(1)} %bitcast.76), channel_id=1, replica_groups=mesh['dp'=16,'emb'=2] {'emb'}, use_global_device_ids=true, to_apply=%region_11.12 | all-reduce | flops 512 | bytes 4096 | tf_op jit(solution)/shard_map/psum | solution.py:73
  58.8 4.7 %fusion.3 = (bf16[512,2048]{1,0:T(8,128)(2,1)S(1)}, bf16[512,2048]{1,0:T(8,128)(2,1)S(1)}) fusion(f32[2048]{0:T(1024)S(1)} %convert_element_type.38, f32[512]{0:T(512)S(1)} %fusion.19, f32[512,2048]{1,0:T(8,128)} %copy-done.2, f32[512,2048]{1,0:T(8,128)} %copy-done.3), kind=kLoop, calls=%fused_computation.12 | loop fusion | flops 14680064 | bytes 12593152 | tf_op jit(solution)/shard_map/convert_element_type | solution.py:79
  63.5 0.7 fusion.33
  64.2 0.6 copy-done.1
  64.8 1.4 convolution_add_fusion
  66.4 3.0 %fusion.32 = f32[128,2048]{1,0:T(8,128)} fusion(bf16[512,128]{1,0:T(8,128)(2,1)S(1)} %all_gather.3, bf16[512,2048]{1,0:T(8,128)(2,1)} %copy-done.1), kind=kOutput, calls=%fused_computation.94 | convolution fusion | flops 268435456 | bytes 3276800 | tf_op jit(solution)/shard_map/dot_general | solution.py:82
  69.4 1.4 fusion.31
  70.9 13.5 %reduce-scatter.2.cloned.1.call-done = f32[256,128]{1,0:T(8,128)} async-done(((f32[512,128]{1,0:T(8,128)}), f32[256,128]{1,0:T(8,128)}) %reduce-scatter.2.cloned.1.call-update) | async-done | bytes 131088 | tf_op jit(solution)/shard_map/reduce_scatter | solution.py:85
  84.4 1.0 fusion.14
  85.4 1.7 fusion.13
  87.2 91.4 %all-reduce.3.cloned.1.call-done = (f32[1536,128]{1,0:T(8,128)}, f32[128,2048]{1,0:T(8,128)}, f32[128,2048]{1,0:T(8,128)}) async-done(((f32[1536,128]{1,0:T(8,128)}, f32[128,2048]{1,0:T(8,128)}, f32[128,2048]{1,0:T(8,128)}), (f32[1536,128]{1,0:T(8,128)}, f32[128,2048]{1,0:T(8,128)}, f32[128,2048]{1,0:T(8,128)})) %all-reduce.3.cloned.1.call-update) | async-done | bytes 2883600 | tf_op jit(solution)/shard_map/psum | solution.py:95
  178.6 3.2 %broadcast_multiply_fusion = (f32[128,2048]{1,0:T(8,128)}, f32[128,2048]{1,0:T(8,128)}) fusion(f32[128,2048]{1,0:T(8,128)} %get-tuple-element.7, f32[128,2048]{1,0:T(8,128)} %get-tuple-element.6), kind=kLoop, calls=%fused_computation.23 | loop fusion | flops 524288 | bytes 4194304 | tf_op jit(solution)/shard_map/mul | solution.py:99
  181.8 1.3 multiply_subtract_fusion
  (45 shorter events, 0.4 us)
Async XLA Ops:
  8.0 43.1 %copy-start = (bf16[128,2048]{1,0:T(8,128)(2,1)S(1)}, bf16[128,2048]{1,0:T(8,128)(2,1)}, u32[]{:S(2)}) copy-start(bf16[128,2048]{1,0:T(8,128)(2,1)} %param.19) | copy-start | bytes 1572868
  8.0 39.2 %copy-start.8 = (f32[128]{0:T(128)S(1)}, f32[128]{0:T(128)}, u32[]{:S(2)}) copy-start(f32[128]{0:T(128)} %param.18) | copy-start | bytes 1540
  13.9 12.6 %all-to-all-start.2 = ((s32[2,1,256]{2,1,0:T(1,128)}), s32[2,1,256]{2,1,0:T(1,128)S(1)}, u32[]{:S(2)}, u32[]{:S(2)}) async-start(s32[2,1,256]{2,1,0:T(1,128)} %bitcast.16), calls=%async_computation.2 | async-start | bytes 4096 | tf_op jit(solution)/shard_map/all_to_all | solution.py:39
  26.5 6.3 %all-to-all-start = ((s32[2,1,256]{2,1,0:T(1,128)}), s32[2,1,256]{2,1,0:T(1,128)S(1)}, u32[]{:S(2)}, u32[]{:S(2)}) async-start(s32[2,1,256]{2,1,0:T(1,128)} %bitcast.6), calls=%async_computation | async-start | bytes 4096 | tf_op jit(solution)/shard_map/all_to_all | solution.py:55
  31.9 19.8 %copy-start.5 = (bf16[128,2048]{1,0:T(8,128)(2,1)S(1)}, bf16[128,2048]{1,0:T(8,128)(2,1)}, u32[]{:S(2)}) copy-start(bf16[128,2048]{1,0:T(8,128)(2,1)} %param.20) | copy-start | bytes 1572868
  32.8 6.7 %all-to-all-start.1 = ((bf16[2,256,128]{2,1,0:T(8,128)(2,1)}), bf16[2,256,128]{2,1,0:T(8,128)(2,1)S(1)}, u32[]{:S(2)}, u32[]{:S(2)}) async-start(bf16[2,256,128]{2,1,0:T(8,128)(2,1)} %bitcast.8), calls=%async_computation.1 | async-start | bytes 262144 | tf_op jit(solution)/shard_map/all_to_all | solution.py:54
  39.5 6.7 %all-to-all-start.3 = ((bf16[2,256,128]{2,1,0:T(8,128)(2,1)}), bf16[2,256,128]{2,1,0:T(8,128)(2,1)S(1)}, u32[]{:S(2)}, u32[]{:S(2)}) async-start(bf16[2,256,128]{2,1,0:T(8,128)(2,1)} %select_convert_fusion), calls=%async_computation.3 | async-start | bytes 262144 | tf_op jit(solution)/shard_map/all_to_all | solution.py:42
  42.9 41.5 %reduce-scatter.2.cloned.1.call-start = ((), (), s32[]{:S(2)}) async-start(), calls=%async_computation.5 | async-start | bytes 393216 | tf_op jit(solution)/shard_map/reduce_scatter | solution.py:85
  51.8 1.9 %copy-start.2 = (f32[512,2048]{1,0:T(8,128)}, f32[512,2048]{1,0:T(8,128)S(1)}, u32[]{:S(2)}) copy-start(f32[512,2048]{1,0:T(8,128)S(1)} %fusion.29) | copy-start | bytes 12582916
  52.5 2.5 %copy-start.3 = (f32[512,2048]{1,0:T(8,128)}, f32[512,2048]{1,0:T(8,128)S(1)}, u32[]{:S(2)}) copy-start(f32[512,2048]{1,0:T(8,128)S(1)} %fusion.30) | copy-start | bytes 12582916
  52.5 6.3 %copy-start.9 = (f32[512]{0:T(512)S(1)}, f32[512]{0:T(512)}, u32[]{:S(2)}) copy-start(f32[512]{0:T(512)} %param.17) | copy-start | bytes 6148
  63.5 1.4 copy-start.1
  66.3 112.3 %all-reduce.3.cloned.1.call-start = ((), (), s32[]{:S(2)}) async-start(), calls=%async_computation.6 | async-start | bytes 5767168 | tf_op jit(solution)/shard_map/psum | solution.py:95
  70.8 111.0 %copy-start.4 = (f32[1536,128]{1,0:T(8,128)S(1)}, f32[1536,128]{1,0:T(8,128)}, u32[]{:S(2)}) copy-start(f32[1536,128]{1,0:T(8,128)} %param.15) | copy-start | bytes 2359300
  70.8 111.0 %copy-start.6 = (f32[1536,128]{1,0:T(8,128)S(1)}, f32[1536,128]{1,0:T(8,128)}, u32[]{:S(2)}) copy-start(f32[1536,128]{1,0:T(8,128)} %param.16) | copy-start | bytes 2359300
  178.6 3.2 %copy-start.7 = (f32[1536,128]{1,0:T(8,128)S(1)}, f32[1536,128]{1,0:T(8,128)}, u32[]{:S(2)}) copy-start(f32[1536,128]{1,0:T(8,128)} %get-tuple-element.5) | copy-start | bytes 2359300
Sparse Core Ops, SparseCore 0:
  66.4 17.9 reduce-scatter.1
Sparse Core Ops, SparseCore 1:
  71.4 107.1 all-reduce.2
where the time goes:
time: 194 us; the launch traced here: 191 us
  waiting for transfers between devices  110 us (57%)
  other arithmetic  17.1 us (9%)
  local copies, waits for them, and re-layouts  16 us (8%)
  between operations  15.8 us (8%)
  starting transfers between devices  13.4 us (7%)
  matrix products  10.7 us (6%)
  blocking collectives  7.53 us (4%)
    psum x1, waiting for transfers between devices, on_device(): lax.psum((gate_part, up_part, table_grad), 'dp')  91.4 us
    reduce_scatter x1, waiting for transfers between devices, on_device(): lax.psum_scatter(result + lax.dot_general(back_up, w_up, across, preferre...  13.5 us
    convert_element_type x1, other arithmetic, on_device(): back_up = (back_hidden * activated).astype(jnp.bfloat16)  4.71 us
  transfers between devices with their start and end apart: 6, of which 5 were waited for; matrix products, arithmetic and copies ran while one was open for 11% of the time, Pallas kernels for 0%

commit v1 on v0

v1 whole, which is shorter than its diff:
```python
import functools
import math

import jax
import jax.numpy as jnp
from jax import lax
from jax.experimental import pallas as pl
from jax.experimental.pallas import tpu as pltpu
from jax.sharding import PartitionSpec as P

loss_weight = 64.0
learn_rate = 0.1
norm_eps = 1e-06
MESH = pl.DeviceIdType.MESH
F32 = jnp.float32
BF16 = jnp.bfloat16


def dot(a, b):
    return jnp.dot(a, b, preferred_element_type=F32)


def dot_nt(a, b):
    return lax.dot_general(a, b, (((1,), (1,)), ((), ())), preferred_element_type=F32)


def tower_kernel(
    n_dp,
    n_emb,
    scale,
    cur_ref,
    prev_ref,
    grads_ref,
    place_ref,
    table_ref,
    labels_ref,
    gain_ref,
    wg_ref,
    wu_ref,
    wo_ref,
    total_ref,
    gate_ref,
    up_ref,
    emb_ref,
    table16,
    posall,
    gall,
    contrib,
    lbuf,
    values,
    normed,
    normed_t,
    act,
    logit,
    logit_in,
    slopes,
    bn,
    bn_in,
    tpart,
    tpair,
    tsum,
    tin,
    tall,
    gpart,
    gpair,
    gsum,
    gin,
    gall_sum,
    e_send,
    e_recv,
    t_send,
    t_recv,
    g_send,
    g_recv,
):
    me_dp = lax.axis_index("dp")
    me_emb = lax.axis_index("emb")
    n_chip = n_dp // 2
    chip = me_dp // 2
    par = me_dp % 2
    other = 1 - par
    partner = me_dp + 1 - 2 * par
    tok = grads_ref.shape[0]
    rows = table_ref.shape[0]
    hid = wg_ref.shape[1]
    ht = 256
    t_rows = rows // n_dp
    g_rows = hid // n_chip

    def copy(src, dst, send, recv, dp, emb):
        return pltpu.make_async_remote_copy(
            src_ref=src,
            dst_ref=dst,
            send_sem=send,
            recv_sem=recv,
            device_id=(dp, emb),
            device_id_type=MESH,
        )

    emb_peers = [lax.rem(me_emb + k, n_emb) for k in range(1, n_emb)]
    chip_peers = [2 * lax.rem(chip + k, n_chip) + par for k in range(1, n_chip)]
    from_chip = [lax.rem(chip + n_chip - k, n_chip) for k in range(1, n_chip)]

    barrier = pltpu.get_barrier_semaphore()
    for peer in emb_peers:
        pl.semaphore_signal(barrier, inc=1, device_id=(me_dp, peer), device_id_type=MESH)
    for peer in chip_peers:
        pl.semaphore_signal(barrier, inc=1, device_id=(peer, me_emb), device_id_type=MESH)
    pl.semaphore_signal(barrier, inc=1, device_id=(partner, me_emb), device_id_type=MESH)

    ids = jnp.concatenate([cur_ref[...], prev_ref[...]], axis=1)
    step = 512

    def place_step(i, acc):
        at = pl.multiple_of(i * step, step)
        part = place_ref[:, pl.ds(at, step)]
        both = jnp.broadcast_to(part, (8, step))
        lane_row = lax.broadcasted_iota(jnp.int32, (8, step), 0)
        halves = jnp.where(lane_row == 0, both >> 6, both & 63).astype(F32).astype(BF16)
        index = lax.broadcasted_iota(jnp.int32, (step, 2 * tok), 0) + at
        hot = jnp.where(index == ids, 1.0, 0.0).astype(BF16)
        return acc + dot(halves, hot)

    found = lax.fori_loop(
        0, place_ref.shape[1] // step, place_step, jnp.zeros((8, 2 * tok), F32)
    )
    pos = (found[0:1, :] * 64.0 + found[1:2, :]).astype(jnp.int32)
    posall[me_emb] = jnp.broadcast_to(pos, (8, 2 * tok))
    gall[me_emb] = grads_ref[...]
    table16[...] = table_ref[...].astype(BF16)
    pl.semaphore_wait(barrier, n_emb - 1 + n_chip - 1 + 1)

    pending = []
    first = []
    for k, peer in enumerate(emb_peers):
        one = copy(
            posall.at[me_emb], posall.at[me_emb], e_send.at[0, k], e_recv.at[0, k], me_dp, peer
        )
        one.start()
        first.append(one)
    second = []
    for k, peer in enumerate(emb_peers):
        one = copy(grads_ref, gall.at[me_emb], e_send.at[1, k], e_recv.at[1, k], me_dp, peer)
        one.start()
        second.append(one)
    pending += first + second
    for one in first:
        one.wait_recv()

    base = me_emb * rows
    kt = 256

    def lookup_step(e, carry):
        line = jnp.broadcast_to(posall[e][0:1, 0:tok] - base, (128, tok)).T
        line = jnp.concatenate([line] * (kt // 128), axis=1)
        acc = jnp.zeros((tok, 128), F32)
        for i in range(rows // kt):
            index = lax.broadcasted_iota(jnp.int32, (tok, kt), 1) + i * kt
            hot = jnp.where(index == line, 1.0, 0.0).astype(BF16)
            acc = acc + dot(hot, table16[i * kt : (i + 1) * kt, :])
        contrib[pl.ds(pl.multiple_of(e * tok, tok), tok), :] = acc.astype(BF16)
        return carry

    lax.fori_loop(0, n_emb, lookup_step, 0)
    third = []
    for k, peer in enumerate(emb_peers):
        one = copy(contrib, lbuf.at[k], e_send.at[2, k], e_recv.at[2, k], me_dp, peer)
        one.start()
        third.append(one)
    pending += third

    for one in second:
        one.wait_recv()
    half_rows = rows // 2
    pt = 128 if half_rows % 128 == 0 else half_rows

    def grad_step(i, carry):
        at = pl.multiple_of(i * pt, pt)
        index = lax.broadcasted_iota(jnp.int32, (pt, tok), 0) + (at + base)
        acc = jnp.zeros((pt, 128), F32)
        for e in range(n_emb):
            hot = jnp.where(index == posall[e][0:1, tok : 2 * tok], 1.0, 0.0).astype(BF16)
            acc = acc + dot(hot, gall[e])
        tpart[pl.ds(at, pt), :] = acc
        return carry

    lax.fori_loop(0, rows // pt, grad_step, 0)
    t_first = copy(
        tpart.at[pl.ds(pl.multiple_of(other * half_rows, 8), half_rows)],
        tpair,
        t_send.at[0, 0],
        t_recv.at[0, 0],
        partner,
        me_emb,
    )
    t_first.start()
    pending.append(t_first)

    for one in third:
        one.wait_recv()
    looked = contrib[...].astype(F32)
    for k in range(n_emb - 1):
        looked = looked + lbuf[k].astype(F32)
    values[...] = looked
    inverse_rms = lax.rsqrt(jnp.mean(looked * looked, axis=1, keepdims=True) + norm_eps)
    norm16 = (looked * inverse_rms * gain_ref[...]).astype(BF16)
    normed[...] = norm16
    normed_t[...] = norm16.astype(F32).T

    logit[...] = jnp.zeros_like(logit)

    def tower_step(j, carry):
        cols = pl.ds(pl.multiple_of(j * ht, ht), ht)
        gate = dot(normed[...], wg_ref[:, cols])
        up = dot(normed[...], wu_ref[:, cols])
        sig = jax.nn.sigmoid(gate)
        activated = gate * sig
        act[0, :, cols] = (up * (sig + activated * (1.0 - sig))).astype(BF16)
        act[1, :, cols] = activated.astype(BF16)
        hidden = (activated * up).astype(BF16)
        head = jnp.broadcast_to(wo_ref[:, cols].astype(F32), (8, ht)).astype(BF16)
        logit[...] += dot_nt(head, hidden)
        return carry

    lax.fori_loop(0, hid // ht, tower_step, 0)
    fourth = []
    for k, peer in enumerate(emb_peers):
        one = copy(logit, logit_in.at[k], e_send.at[3, k], e_recv.at[3, k], me_dp, peer)
        one.start()
        fourth.append(one)
    pending += fourth

    t_first.wait_recv()
    tsum[...] = tpart[pl.ds(pl.multiple_of(par * half_rows, 8), half_rows), :] + tpair[...]
    t_scatter = []
    for k, peer in enumerate(chip_peers):
        there = pl.multiple_of(lax.rem(chip + k + 1, n_chip) * t_rows, 8)
        one = copy(
            tsum.at[pl.ds(there, t_rows)],
            tin.at[k],
            t_send.at[1, k],
            t_recv.at[1, k],
            peer,
            me_emb,
        )
        one.start()
        t_scatter.append(one)
    pending += t_scatter

    bn[...] = jnp.zeros_like(bn)

    def back_step(j, carry):
        cols = pl.ds(pl.multiple_of(j * ht, ht), ht)
        head = wo_ref[:, cols].astype(F32)
        wg = (wg_ref[:, cols].astype(F32) * head).astype(BF16)
        wu = (wu_ref[:, cols].astype(F32) * head).astype(BF16)
        bn[...] += dot_nt(act[0, :, cols], wg) + dot_nt(act[1, :, cols], wu)
        return carry

    lax.fori_loop(0, hid // ht, back_step, 0)
    fifth = []
    for k, peer in enumerate(emb_peers):
        one = copy(
            bn.at[pl.ds(pl.multiple_of(peer * tok, tok), tok)],
            bn_in.at[k],
            e_send.at[4, k],
            e_recv.at[4, k],
            me_dp,
            peer,
        )
        one.start()
        fifth.append(one)
    pending += fifth

    for one in fourth:
        one.wait_recv()
    logits = logit[...]
    for k in range(n_emb - 1):
        logits = logits + logit_in[k]
    slope = loss_weight * (jax.nn.sigmoid(logits) - labels_ref[...])
    slopes[...] = slope
    lead = (normed_t[...] * slope[0:1, :]).astype(BF16)

    def weight_grads(which):
        for j in range(hid // ht):
            cols = slice(j * ht, (j + 1) * ht)
            head = wo_ref[:, cols].astype(F32) * scale
            part = (dot(lead, act[which, :, cols]) * head).astype(BF16)
            for b in range(ht // 128):
                at = j * ht + b * 128
                gpart[which, at : at + 128, :] = part[:, b * 128 : (b + 1) * 128]

    weight_grads(other)
    g_first = copy(gpart.at[other], gpair, g_send.at[0, 0], g_recv.at[0, 0], partner, me_emb)
    g_first.start()
    pending.append(g_first)
    weight_grads(par)

    for one in t_scatter:
        one.wait_recv()
    piece = tsum[pl.ds(pl.multiple_of(chip * t_rows, 8), t_rows), :]
    for k in range(n_chip - 1):
        piece = piece + tin[k]
    mine = pl.ds(pl.multiple_of(par * half_rows + chip * t_rows, 8), t_rows)
    tall[mine, :] = piece
    t_spread = []
    for k, peer in enumerate(chip_peers):
        one = copy(
            tall.at[mine], tall.at[mine], t_send.at[2, k], t_recv.at[2, k], peer, me_emb
        )
        one.start()
        t_spread.append(one)
    t_last = [
        copy(
            tall.at[mine],
            tall.at[mine],
            t_send.at[3, n_chip - 1],
            t_recv.at[3, n_chip - 1],
            partner,
            me_emb,
        )
    ]
    t_last[0].start()

    g_first.wait_recv()
    gsum[...] = (gpart[par].astype(F32) + gpair[...].astype(F32)).astype(BF16)
    g_scatter = []
    for k, peer in enumerate(chip_peers):
        there = pl.multiple_of(lax.rem(chip + k + 1, n_chip) * g_rows, 16)
        one = copy(
            gsum.at[pl.ds(there, g_rows)],
            gin.at[k],
            g_send.at[1, k],
            g_recv.at[1, k],
            peer,
            me_emb,
        )
        one.start()
        g_scatter.append(one)
    pending += g_scatter

    for one in fifth:
        one.wait_recv()
    own = pl.ds(pl.multiple_of(me_emb * tok, tok), tok)
    back = bn[own, :]
    for k in range(n_emb - 1):
        back = back + bn_in[k]
    slope_col = jnp.broadcast_to(slopes[0:1, own], (128, tok)).T
    scaled = back * slope_col * gain_ref[...]
    x = values[own, :]
    inv = lax.rsqrt(jnp.mean(x * x, axis=1, keepdims=True) + norm_eps)
    emb_ref[...] = inv * scaled - x * (inv * inv * inv) * jnp.mean(
        x * scaled, axis=1, keepdims=True
    )

    for k in range(n_chip - 1):
        t_spread[k].wait_recv()
        came = pl.ds(
            pl.multiple_of(par * half_rows + from_chip[k] * t_rows, 8), t_rows
        )
        one = copy(
            tall.at[came], tall.at[came], t_send.at[3, k], t_recv.at[3, k], partner, me_emb
        )
        one.start()
        t_last.append(one)
    pending += t_spread + t_last

    for one in g_scatter:
        one.wait_recv()
    piece = gsum[pl.ds(pl.multiple_of(chip * g_rows, 16), g_rows), :].astype(F32)
    for k in range(n_chip - 1):
        piece = piece + gin[k].astype(F32)
    mine = pl.ds(pl.multiple_of(chip * g_rows, 16), g_rows)
    gall_sum[par, mine, :] = piece.astype(BF16)
    g_spread = []
    for k, peer in enumerate(chip_peers):
        one = copy(
            gall_sum.at[par, mine],
            gall_sum.at[par, mine],
            g_send.at[2, k],
            g_recv.at[2, k],
            peer,
            me_emb,
        )
        one.start()
        g_spread.append(one)
    g_last = [
        copy(
            gall_sum.at[par, mine],
            gall_sum.at[par, mine],
            g_send.at[3, n_chip - 1],
            g_recv.at[3, n_chip - 1],
            partner,
            me_emb,
        )
    ]
    g_last[0].start()
    for one in t_last:
        one.wait_recv()
    total_ref[...] = tall[...]
    for k in range(n_chip - 1):
        g_spread[k].wait_recv()
        came = pl.ds(pl.multiple_of(from_chip[k] * g_rows, 16), g_rows)
        one = copy(
            gall_sum.at[par, came],
            gall_sum.at[par, came],
            g_send.at[3, k],
            g_recv.at[3, k],
            partner,
            me_emb,
        )
        one.start()
        g_last.append(one)
    pending += g_spread + g_last
    for one in g_last:
        one.wait_recv()
    for b in range(hid // 128):
        cols = slice(b * 128, (b + 1) * 128)
        gate_ref[:, cols] = gall_sum[0, cols, :]
        up_ref[:, cols] = gall_sum[1, cols, :]
    for one in pending:
        one.wait_send()


def on_device(
    cur_ids, prev_ids, prev_grads, row_place, table, accum, labels, gain, w_gate, w_up, w_out
):
    n_emb = lax.axis_size("emb")
    n_dp = lax.axis_size("dp")
    n_chip = n_dp // 2
    rows, width = table.shape
    tok = cur_ids.shape[0]
    group = tok * n_emb
    hid = w_gate.shape[1]
    scale = 1.0 / math.sqrt(tok * n_emb * n_dp)
    vmem = pl.BlockSpec(memory_space=pltpu.VMEM)
    n_peer = max(n_emb - 1, 1)
    dma = pltpu.SemaphoreType.DMA
    total, gate, up, emb_grad = pl.pallas_call(
        functools.partial(tower_kernel, n_dp, n_emb, scale),
        out_shape=(
            jax.ShapeDtypeStruct((rows, width), F32),
            jax.ShapeDtypeStruct((width, hid), BF16),
            jax.ShapeDtypeStruct((width, hid), BF16),
            jax.ShapeDtypeStruct((tok, width), F32),
        ),
        in_specs=[vmem] * 10,
        out_specs=(vmem,) * 4,
        scratch_shapes=[
            pltpu.VMEM((rows, width), BF16),
            pltpu.VMEM((n_emb, 8, 2 * tok), jnp.int32),
            pltpu.VMEM((n_emb, tok, width), BF16),
            pltpu.VMEM((group, width), BF16),
            pltpu.VMEM((n_peer, group, width), BF16),
            pltpu.VMEM((group, width), F32),
            pltpu.VMEM((group, width), BF16),
            pltpu.VMEM((width, group), F32),
            pltpu.VMEM((2, group, hid), BF16),
            pltpu.VMEM((8, group), F32),
            pltpu.VMEM((n_peer, 8, group), F32),
            pltpu.VMEM((8, group), F32),
            pltpu.VMEM((group, width), F32),
            pltpu.VMEM((n_peer, tok, width), F32),
            pltpu.VMEM((rows, width), F32),
            pltpu.VMEM((rows // 2, width), F32),
            pltpu.VMEM((rows // 2, width), F32),
            pltpu.VMEM((n_chip - 1, rows // n_dp, width), F32),
            pltpu.VMEM((rows, width), F32),
            pltpu.VMEM((2, hid, width), BF16),
            pltpu.VMEM((hid, width), BF16),
            pltpu.VMEM((hid, width), BF16),
            pltpu.VMEM((n_chip - 1, hid // n_chip, width), BF16),
            pltpu.VMEM((2, hid, width), BF16),
            dma((5, n_peer)),
            dma((5, n_peer)),
            dma((4, n_chip)),
            dma((4, n_chip)),
            dma((4, n_chip)),
            dma((4, n_chip)),
        ],
        compiler_params=pltpu.CompilerParams(
            collective_id=0, has_side_effects=True, vmem_limit_bytes=60 * 1024 * 1024
        ),
    )(
        cur_ids.reshape(1, -1),
        prev_ids.reshape(1, -1),
        prev_grads,
        row_place.reshape(1, -1),
        table,
        labels.reshape(1, -1),
        gain.reshape(1, -1),
        w_gate,
        w_up,
        w_out.reshape(1, -1),
    )
    new_accum = accum + total * total
    new_table = table - learn_rate * total * lax.rsqrt(new_accum)
    return (new_table, new_accum, gate.astype(F32), up.astype(F32), emb_grad)


def solution(mesh):
    placed = (
        P(("dp", "emb")),
        P(("dp", "emb")),
        P(("dp", "emb"), None),
        P(),
        P("emb", None),
        P("emb", None),
        P("dp"),
        P(),
        P(None, "emb"),
        P(None, "emb"),
        P("emb"),
    )
    return jax.shard_map(
        on_device,
        mesh=mesh,
        in_specs=placed,
        out_specs=(
            P("emb", None),
            P("emb", None),
            P(None, "emb"),
            P(None, "emb"),
            P(("dp", "emb"), None),
        ),
        check_vma=False,
    )
```

time: 194 us -> 70.7 us (0.36); the launches traced: 191 us -> 70.5 us
  waiting for transfers between devices: 110 us -> 0 us
  Pallas kernels: 0 us -> 63.2 us
  between operations: 15.8 us -> 0.68 us
  local copies, waits for them, and re-layouts: 16 us -> 2.02 us
  starting transfers between devices: 13.4 us -> 0 us
  other arithmetic: 17.1 us -> 4.62 us
  matrix products: 10.7 us -> 0 us
  blocking collectives: 7.53 us -> 0 us
    psum x1 -> x0, waiting for transfers between devices: 91.4 us -> none  [on_device(): lax.psum((gate_part, up_part, table_grad), 'dp')]
    pallas_call x0 -> x1, Pallas kernels: none -> 63.2 us  [on_device(): pl.pallas_call(functools.partial(tower_kernel, n_dp, n_emb, scale), out_s...]
    reduce_scatter x1 -> x0, waiting for transfers between devices: 13.5 us -> none  [on_device(): lax.psum_scatter(result + lax.dot_general(back_up, w_up, across, preferre...]
    all_to_all x4 -> x0, starting transfers between devices: 13.3 us -> none  [the longest x1 3.38 us: on_device(): lax.all_to_all(grad_pack, 'emb', split_axis=0, concat_axis=0, tiled=True)]
    dot_general x8 -> x0, matrix products: 10.7 us -> none  [the longest x1 3.04 us: on_device(): lax.dot_general(gathered, back_up, contract, preferred_element_type=jnp.f...]
    gather x4 -> x0, local copies, waits for them, and re-layouts: 6.93 us -> none  [the longest x1 2.19 us: on_device(): fetched = table[jnp.maximum(wanted, 0)]]
    scatter x3 -> x0, local copies, waits for them, and re-layouts: 6 us -> none  [the longest x1 2.09 us: on_device(): jnp.zeros((shards * capacity, emb_width), jnp.bfloat16).at[grad_pos]]
    all_to_all x4 -> x0, waiting for transfers between devices: 5.14 us -> none  [the longest x1 2.51 us: on_device(): lax.all_to_all(grad_pack, 'emb', split_axis=0, concat_axis=0, tiled=True)]
  transfers between devices with their start and end apart: 6 -> 0, of which waited for: 5 -> 0; matrix products, arithmetic and copies ran while one was open for 11% -> 0% of each run, Pallas kernels for 0% -> 0%
where the time goes in v1:
time: 70.7 us; the launch traced here: 70.5 us
  Pallas kernels  63.2 us (89%)
  other arithmetic  4.62 us (7%)
  local copies, waits for them, and re-layouts  2.02 us (3%)
    pallas_call x1, Pallas kernels, on_device(): pl.pallas_call(functools.partial(tower_kernel, n_dp, n_emb, scale), out_s...  63.2 us
    sub x1, other arithmetic, on_device(): new_table = table - learn_rate * total * lax.rsqrt(new_accum)  2.48 us
    convert_element_type x2, other arithmetic, on_device(): return (new_table, new_accum, gate.astype(F32), up.astype(F32), emb_grad)  2.14 us

profile of v1, /device:TPU:1, one launch (start us, length us, event | category | flops | bytes accessed | tf_op | source)
XLA Modules:
  0.0 70.5 jit_solution(4564111958004662318)
XLA Ops:
  0.6 0.0 copy-start.5
  0.6 0.7 copy-done.5
  1.3 0.6 reshape.33.wo_ref
  1.9 0.0 copy-start
  1.9 0.0 copy-start.1
  1.9 63.2 %shard_map.146 = (f32[1536,128]{1,0:T(8,128)}, bf16[128,2048]{1,0:T(8,128)(2,1)}, bf16[128,2048]{1,0:T(8,128)(2,1)}, f32[256,128]{1,0:T(8,128)}) custom-call(s32[1,256]{1,0:T(1,128)} %bitcast.7, s32[1,256]{1,0:T(1,128)} %bitcast.8, bf16[256,128]{1,0:T(8,128)(2,1)} %grads_ref.1, s32[1,3072]{1,0:T(1,128)} %bitcast.5, f32[1536,128]{1,0:T(8,128)} %table_ref.1, ...), custom_call_target="tpu_custom_call" | custom-call | tf_op jit(solution)/shard_map/pallas_call | solution.py:439
  65.1 0.0 copy-done
  65.1 0.0 copy-done.1
  65.1 0.0 copy-start.3
  65.1 2.5 %multiply_subtract_fusion = (f32[1536,128]{1,0:T(8,128)}, f32[1536,128]{1,0:T(8,128)}) fusion(f32[1536,128]{1,0:T(8,128)S(1)} %copy-done, f32[1536,128]{1,0:T(8,128)} %get-tuple-element.9, f32[1536,128]{1,0:T(8,128)S(1)} %copy-done.1), kind=kLoop, calls=%fused_computation | loop fusion | flops 983040 | bytes 3932160 | tf_op jit(solution)/shard_map/sub | solution.py:497
  67.6 0.0 copy-done.3
  67.6 0.0 copy-start.2
  67.6 1.1 %convert_element_type.6 = f32[128,2048]{1,0:T(8,128)} convert(bf16[128,2048]{1,0:T(8,128)(2,1)S(1)} %copy-done.3) | non-fusion elementwise | flops 262144 | bytes 1572864 | tf_op jit(solution)/shard_map/convert_element_type | solution.py:498
  68.7 0.1 copy-done.2
  68.8 0.0 copy-start.4
  68.8 1.1 %convert_element_type.7 = f32[128,2048]{1,0:T(8,128)} convert(bf16[128,2048]{1,0:T(8,128)(2,1)S(1)} %copy-done.2) | non-fusion elementwise | flops 262144 | bytes 1572864 | tf_op jit(solution)/shard_map/convert_element_type | solution.py:498
  69.8 0.0 copy-done.4
  69.8 0.7 copy.17
Async XLA Ops:
  0.6 0.7 copy-start.5
  1.9 63.2 %copy-start = (f32[1536,128]{1,0:T(8,128)S(1)}, f32[1536,128]{1,0:T(8,128)}, u32[]{:S(2)}) copy-start(f32[1536,128]{1,0:T(8,128)} %table_ref.1) | copy-start | bytes 2359300
  1.9 63.2 %copy-start.1 = (f32[1536,128]{1,0:T(8,128)S(1)}, f32[1536,128]{1,0:T(8,128)}, u32[]{:S(2)}) copy-start(f32[1536,128]{1,0:T(8,128)} %param.16) | copy-start | bytes 2359300
  65.1 2.5 %copy-start.3 = (bf16[128,2048]{1,0:T(8,128)(2,1)S(1)}, bf16[128,2048]{1,0:T(8,128)(2,1)}, u32[]{:S(2)}) copy-start(bf16[128,2048]{1,0:T(8,128)(2,1)} %get-tuple-element.10) | copy-start | bytes 1572868
  67.6 1.1 %copy-start.2 = (bf16[128,2048]{1,0:T(8,128)(2,1)S(1)}, bf16[128,2048]{1,0:T(8,128)(2,1)}, u32[]{:S(2)}) copy-start(bf16[128,2048]{1,0:T(8,128)(2,1)} %get-tuple-element.11) | copy-start | bytes 1572868
  68.8 1.1 %copy-start.4 = (f32[256,128]{1,0:T(8,128)S(1)}, f32[256,128]{1,0:T(8,128)}, u32[]{:S(2)}) copy-start(f32[256,128]{1,0:T(8,128)} %get-tuple-element.24) | copy-start | bytes 393220

commit v2 on v1

--- a/solution.py
+++ b/solution.py
@@ -59,13 +59,17 @@
     tpart,
     tpair,
     tsum,
-    tin,
+    tx_in,
+    tz_out,
+    tz_in,
     tall,
     gpart,
     gpair,
     gsum,
-    gin,
-    gall_sum,
+    gx_in,
+    gz_out,
+    gz_in,
+    gtotal,
     e_send,
     e_recv,
     t_send,
@@ -76,16 +80,18 @@
     me_dp = lax.axis_index("dp")
     me_emb = lax.axis_index("emb")
     n_chip = n_dp // 2
+    n_hi = n_chip // 2
     chip = me_dp // 2
+    low = chip % 2
+    high = chip // 2
     par = me_dp % 2
     other = 1 - par
     partner = me_dp + 1 - 2 * par
+    beside = me_dp + 2 - 4 * low
     tok = grads_ref.shape[0]
     rows = table_ref.shape[0]
     hid = wg_ref.shape[1]
     ht = 256
-    t_rows = rows // n_dp
-    g_rows = hid // n_chip
 
     def copy(src, dst, send, recv, dp, emb):
         return pltpu.make_async_remote_copy(
@@ -98,13 +104,99 @@
         )
 
     emb_peers = [lax.rem(me_emb + k, n_emb) for k in range(1, n_emb)]
-    chip_peers = [2 * lax.rem(chip + k, n_chip) + par for k in range(1, n_chip)]
-    from_chip = [lax.rem(chip + n_chip - k, n_chip) for k in range(1, n_chip)]
+    ahead = [lax.rem(high + k, n_hi) for k in range(n_hi)]
+    behind = [lax.rem(high + n_hi - k, n_hi) for k in range(n_hi)]
+    far_peers = [(2 * h + low) * 2 + par for h in ahead]
+    pending = []
+
+    class Reduce:
+
+        def __init__(self, part, pair, acc, x_in, z_out, z_in, full, send, recv, align):
+            self.part, self.pair, self.acc, self.x_in = part, pair, acc, x_in
+            self.z_out, self.z_in, self.full = z_out, z_in, full
+            self.send, self.recv, self.align = send, recv, align
+            self.half = pair.shape[0]
+            self.size = self.half // n_chip
+
+        def rows(self, at, size):
+            return pl.ds(pl.multiple_of(at, self.align), size)
+
+        def piece(self, lo, hi):
+            return self.rows((lo * n_hi + hi) * self.size, self.size)
+
+        def place(self, lo, hi):
+            return self.rows(par * self.half + (lo * n_hi + hi) * self.size, self.size)
+
+        def go(self, src, dst, stage, k, dp):
+            one = copy(src, dst, self.send.at[stage, k], self.recv.at[stage, k], dp, me_emb)
+            one.start()
+            pending.append(one)
+            return one
+
+        def start(self):
+            away = self.rows(other * self.half, self.half)
+            self.first = self.go(self.part.at[away], self.pair, 0, 0, partner)
+
+        def stage_x(self):
+            self.first.wait_recv()
+            kept = self.part[self.rows(par * self.half, self.half), :]
+            joined = kept.astype(F32) + self.pair[...].astype(F32)
+            self.acc[...] = joined.astype(self.acc.dtype)
+            self.x = {}
+            for k in list(range(1, n_hi)) + [0]:
+                self.x[k] = self.go(
+                    self.acc.at[self.piece(1 - low, ahead[k])], self.x_in.at[k], 1, k, beside
+                )
+
+        def joined(self, k):
+            self.x[k].wait_recv()
+            kept = self.acc[self.piece(low, ahead[k]), :].astype(F32)
+            return kept + self.x_in[k].astype(F32)
+
+        def stage_z(self):
+            self.z = []
+            for k in range(1, n_hi):
+                self.z_out[k - 1] = self.joined(k).astype(self.z_out.dtype)
+                self.z.append(
+                    self.go(self.z_out.at[k - 1], self.z_in.at[k - 1], 2, k, far_peers[k])
+                )
+
+        def stage_sum(self):
+            total = self.joined(0)
+            for k, one in enumerate(self.z):
+                one.wait_recv()
+                total = total + self.z_in[k].astype(F32)
+            mine = self.place(low, high)
+            self.full[mine, :] = total.astype(self.full.dtype)
+            view = self.full.at[mine]
+            self.far = [self.go(view, view, 3, k, far_peers[k]) for k in range(1, n_hi)]
+            self.near = [self.go(view, view, 4, 0, beside)]
+            self.last = [self.go(view, view, 5, 0, partner)]
+
+        def spread_z(self):
+            for k in range(1, n_hi):
+                self.far[k - 1].wait_recv()
+                view = self.full.at[self.place(low, behind[k])]
+                self.near.append(self.go(view, view, 4, k, beside))
+                self.last.append(self.go(view, view, 5, k, partner))
+
+        def spread_x(self):
+            for k in range(n_hi):
+                self.near[k].wait_recv()
+                view = self.full.at[self.place(1 - low, behind[k])]
+                self.last.append(self.go(view, view, 5, n_hi + k, partner))
+
+        def finish(self):
+            for one in self.last:
+                one.wait_recv()
+
+    sums = Reduce(tpart, tpair, tsum, tx_in, tz_out, tz_in, tall, t_send, t_recv, 8)
+    tower = Reduce(gpart, gpair, gsum, gx_in, gz_out, gz_in, gtotal, g_send, g_recv, 16)
 
     barrier = pltpu.get_barrier_semaphore()
     for peer in emb_peers:
         pl.semaphore_signal(barrier, inc=1, device_id=(me_dp, peer), device_id_type=MESH)
-    for peer in chip_peers:
+    for peer in far_peers[1:] + [beside]:
         pl.semaphore_signal(barrier, inc=1, device_id=(peer, me_emb), device_id_type=MESH)
     pl.semaphore_signal(barrier, inc=1, device_id=(partner, me_emb), device_id_type=MESH)
 
@@ -128,9 +220,8 @@
     posall[me_emb] = jnp.broadcast_to(pos, (8, 2 * tok))
     gall[me_emb] = grads_ref[...]
     table16[...] = table_ref[...].astype(BF16)
-    pl.semaphore_wait(barrier, n_emb - 1 + n_chip - 1 + 1)
-
-    pending = []
+    pl.semaphore_wait(barrier, n_emb - 1 + n_hi - 1 + 2)
+
     first = []
     for k, peer in enumerate(emb_peers):
         one = copy(
@@ -185,16 +276,8 @@
         return carry
 
     lax.fori_loop(0, rows // pt, grad_step, 0)
-    t_first = copy(
-        tpart.at[pl.ds(pl.multiple_of(other * half_rows, 8), half_rows)],
-        tpair,
-        t_send.at[0, 0],
-        t_recv.at[0, 0],
-        partner,
-        me_emb,
-    )
-    t_first.start()
-    pending.append(t_first)
+    sums.start()
+    sums.stage_x()
 
     for one in third:
         one.wait_recv()
@@ -222,30 +305,17 @@
         logit[...] += dot_nt(head, hidden)
         return carry
 
-    lax.fori_loop(0, hid // ht, tower_step, 0)
+    tiles = hid // ht
+    some = max(1, 5 * tiles // 8)
+    lax.fori_loop(0, some, tower_step, 0)
+    sums.stage_z()
+    lax.fori_loop(some, tiles, tower_step, 0)
     fourth = []
     for k, peer in enumerate(emb_peers):
         one = copy(logit, logit_in.at[k], e_send.at[3, k], e_recv.at[3, k], me_dp, peer)
         one.start()
         fourth.append(one)
     pending += fourth
-
-    t_first.wait_recv()
-    tsum[...] = tpart[pl.ds(pl.multiple_of(par * half_rows, 8), half_rows), :] + tpair[...]
-    t_scatter = []
-    for k, peer in enumerate(chip_peers):
-        there = pl.multiple_of(lax.rem(chip + k + 1, n_chip) * t_rows, 8)
-        one = copy(
-            tsum.at[pl.ds(there, t_rows)],
-            tin.at[k],
-            t_send.at[1, k],
-            t_recv.at[1, k],
-            peer,
-            me_emb,
-        )
-        one.start()
-        t_scatter.append(one)
-    pending += t_scatter
 
     bn[...] = jnp.zeros_like(bn)
 
@@ -288,56 +358,13 @@
             part = (dot(lead, act[which, :, cols]) * head).astype(BF16)
             for b in range(ht // 128):
                 at = j * ht + b * 128
-                gpart[which, at : at + 128, :] = part[:, b * 128 : (b + 1) * 128]
+                gpart[pl.ds(pl.multiple_of(which * hid + at, 128), 128), :] = part[:, b * 128 : (b + 1) * 128]
 
     weight_grads(other)
-    g_first = copy(gpart.at[other], gpair, g_send.at[0, 0], g_recv.at[0, 0], partner, me_emb)
-    g_first.start()
-    pending.append(g_first)
+    tower.start()
+    sums.stage_sum()
     weight_grads(par)
-
-    for one in t_scatter:
-        one.wait_recv()
-    piece = tsum[pl.ds(pl.multiple_of(chip * t_rows, 8), t_rows), :]
-    for k in range(n_chip - 1):
-        piece = piece + tin[k]
-    mine = pl.ds(pl.multiple_of(par * half_rows + chip * t_rows, 8), t_rows)
-    tall[mine, :] = piece
-    t_spread = []
-    for k, peer in enumerate(chip_peers):
-        one = copy(
-            tall.at[mine], tall.at[mine], t_send.at[2, k], t_recv.at[2, k], peer, me_emb
-        )
-        one.start()
-        t_spread.append(one)
-    t_last = [
-        copy(
-            tall.at[mine],
-            tall.at[mine],
-            t_send.at[3, n_chip - 1],
-            t_recv.at[3, n_chip - 1],
-            partner,
-            me_emb,
-        )
-    ]
-    t_last[0].start()
-
-    g_first.wait_recv()
-    gsum[...] = (gpart[par].astype(F32) + gpair[...].astype(F32)).astype(BF16)
-    g_scatter = []
-    for k, peer in enumerate(chip_peers):
-        there = pl.multiple_of(lax.rem(chip + k + 1, n_chip) * g_rows, 16)
-        one = copy(
-            gsum.at[pl.ds(there, g_rows)],
-            gin.at[k],
-            g_send.at[1, k],
-            g_recv.at[1, k],
-            peer,
-            me_emb,
-        )
-        one.start()
-        g_scatter.append(one)
-    pending += g_scatter
+    tower.stage_x()
 
     for one in fifth:
         one.wait_recv()
@@ -353,71 +380,19 @@
         x * scaled, axis=1, keepdims=True
     )
 
-    for k in range(n_chip - 1):
-        t_spread[k].wait_recv()
-        came = pl.ds(
-            pl.multiple_of(par * half_rows + from_chip[k] * t_rows, 8), t_rows
-        )
-        one = copy(
-            tall.at[came], tall.at[came], t_send.at[3, k], t_recv.at[3, k], partner, me_emb
-        )
-        one.start()
-        t_last.append(one)
-    pending += t_spread + t_last
-
-    for one in g_scatter:
-        one.wait_recv()
-    piece = gsum[pl.ds(pl.multiple_of(chip * g_rows, 16), g_rows), :].astype(F32)
-    for k in range(n_chip - 1):
-        piece = piece + gin[k].astype(F32)
-    mine = pl.ds(pl.multiple_of(chip * g_rows, 16), g_rows)
-    gall_sum[par, mine, :] = piece.astype(BF16)
-    g_spread = []
-    for k, peer in enumerate(chip_peers):
-        one = copy(
-            gall_sum.at[par, mine],
-            gall_sum.at[par, mine],
-            g_send.at[2, k],
-            g_recv.at[2, k],
-            peer,
-            me_emb,
-        )
-        one.start()
-        g_spread.append(one)
-    g_last = [
-        copy(
-            gall_sum.at[par, mine],
-            gall_sum.at[par, mine],
-            g_send.at[3, n_chip - 1],
-            g_recv.at[3, n_chip - 1],
-            partner,
-            me_emb,
-        )
-    ]
-    g_last[0].start()
-    for one in t_last:
-        one.wait_recv()
+    tower.stage_z()
+    sums.spread_z()
+    tower.stage_sum()
+    sums.spread_x()
+    tower.spread_z()
+    tower.spread_x()
+    sums.finish()
     total_ref[...] = tall[...]
-    for k in range(n_chip - 1):
-        g_spread[k].wait_recv()
-        came = pl.ds(pl.multiple_of(from_chip[k] * g_rows, 16), g_rows)
-        one = copy(
-            gall_sum.at[par, came],
-            gall_sum.at[par, came],
-            g_send.at[3, k],
-            g_recv.at[3, k],
-            partner,
-            me_emb,
-        )
-        one.start()
-        g_last.append(one)
-    pending += g_spread + g_last
-    for one in g_last:
-        one.wait_recv()
+    tower.finish()
     for b in range(hid // 128):
         cols = slice(b * 128, (b + 1) * 128)
-        gate_ref[:, cols] = gall_sum[0, cols, :]
-        up_ref[:, cols] = gall_sum[1, cols, :]
+        gate_ref[:, cols] = gtotal[cols, :]
+        up_ref[:, cols] = gtotal[hid + b * 128 : hid + (b + 1) * 128, :]
     for one in pending:
         one.wait_send()
 
@@ -428,6 +403,7 @@
     n_emb = lax.axis_size("emb")
     n_dp = lax.axis_size("dp")
     n_chip = n_dp // 2
+    n_hi = n_chip // 2
     rows, width = table.shape
     tok = cur_ids.shape[0]
     group = tok * n_emb
@@ -464,19 +440,23 @@
             pltpu.VMEM((rows, width), F32),
             pltpu.VMEM((rows // 2, width), F32),
             pltpu.VMEM((rows // 2, width), F32),
-            pltpu.VMEM((n_chip - 1, rows // n_dp, width), F32),
+            pltpu.VMEM((n_hi, rows // n_dp, width), F32),
+            pltpu.VMEM((n_hi - 1, rows // n_dp, width), F32),
+            pltpu.VMEM((n_hi - 1, rows // n_dp, width), F32),
             pltpu.VMEM((rows, width), F32),
-            pltpu.VMEM((2, hid, width), BF16),
+            pltpu.VMEM((2 * hid, width), BF16),
             pltpu.VMEM((hid, width), BF16),
             pltpu.VMEM((hid, width), BF16),
-            pltpu.VMEM((n_chip - 1, hid // n_chip, width), BF16),
-            pltpu.VMEM((2, hid, width), BF16),
+            pltpu.VMEM((n_hi, hid // n_chip, width), BF16),
+            pltpu.VMEM((n_hi - 1, hid // n_chip, width), BF16),
+            pltpu.VMEM((n_hi - 1, hid // n_chip, width), BF16),
+            pltpu.VMEM((2 * hid, width), BF16),
             dma((5, n_peer)),
             dma((5, n_peer)),
-            dma((4, n_chip)),
-            dma((4, n_chip)),
-            dma((4, n_chip)),
-            dma((4, n_chip)),
+            dma((6, 2 * n_hi)),
+            dma((6, 2 * n_hi)),
+            dma((6, 2 * n_hi)),
+            dma((6, 2 * n_hi)),
         ],
         compiler_params=pltpu.CompilerParams(
             collective_id=0, has_side_effects=True, vmem_limit_bytes=60 * 1024 * 1024

time: 70.7 us -> 57.4 us (0.81)
  Pallas kernels: 63.2 us -> 49.8 us
    pallas_call x1, Pallas kernels: 63.2 us -> 49.8 us  [on_device(): pl.pallas_call(functools.partial(tower_kernel, n_dp, n_emb, scale), out_s...]
where the time goes in v2:
time: 57.4 us; the launch traced here: 57.1 us
  Pallas kernels  49.8 us (87%)
  other arithmetic  4.62 us (8%)
  local copies, waits for them, and re-layouts  2.02 us (4%)
  between operations  0.68 us (1%)
    pallas_call x1, Pallas kernels, on_device(): pl.pallas_call(functools.partial(tower_kernel, n_dp, n_emb, scale), out_s...  49.8 us
    sub x1, other arithmetic, on_device(): new_table = table - learn_rate * total * lax.rsqrt(new_accum)  2.48 us
    convert_element_type x2, other arithmetic, on_device(): return (new_table, new_accum, gate.astype(F32), up.astype(F32), emb_grad)  2.14 us
    unnamed x13, local copies, waits for them, and re-layouts  1.41 us

profile of v2, /device:TPU:1, one launch (start us, length us, event | category | flops | bytes accessed | tf_op | source)
XLA Modules:
  0.0 57.1 jit_solution(8765689456496155141)
XLA Ops:
  0.6 0.0 copy-start.5
  0.6 0.7 %copy-done.5 = bf16[2048]{0:T(1024)(128)(2,1)S(1)} copy-done((bf16[2048]{0:T(1024)(128)(2,1)S(1)}, bf16[2048]{0:T(1024)(128)(2,1)}, u32[]{:S(2)}) %copy-start.5) | copy-done | bytes 4120
  1.3 0.6 %reshape.33.wo_ref = bf16[1,2048]{1,0:T(2,128)(2,1)} reshape(bf16[2048]{0:T(1024)(128)(2,1)S(1)} %copy-done.5) | data formatting | bytes 8192 | tf_op jit(solution)/shard_map/reshape | solution.py:474
  1.9 0.0 copy-start
  1.9 0.0 copy-start.1
  1.9 49.8 %shard_map.146 = (f32[1536,128]{1,0:T(8,128)}, bf16[128,2048]{1,0:T(8,128)(2,1)}, bf16[128,2048]{1,0:T(8,128)(2,1)}, f32[256,128]{1,0:T(8,128)}) custom-call(s32[1,256]{1,0:T(1,128)} %bitcast.7, s32[1,256]{1,0:T(1,128)} %bitcast.8, bf16[256,128]{1,0:T(8,128)(2,1)} %grads_ref.1, s32[1,3072]{1,0:T(1,128)} %bitcast.5, f32[1536,128]{1,0:T(8,128)} %table_ref.1, ...), custom_call_target="tpu_custom_call" | custom-call | tf_op jit(solution)/shard_map/pallas_call | solution.py:415
  51.8 0.0 copy-done
  51.8 0.0 copy-done.1
  51.8 0.0 copy-start.3
  51.8 2.5 %multiply_subtract_fusion = (f32[1536,128]{1,0:T(8,128)}, f32[1536,128]{1,0:T(8,128)}) fusion(f32[1536,128]{1,0:T(8,128)S(1)} %copy-done, f32[1536,128]{1,0:T(8,128)} %get-tuple-element.9, f32[1536,128]{1,0:T(8,128)S(1)} %copy-done.1), kind=kLoop, calls=%fused_computation | loop fusion | flops 983040 | bytes 3932160 | tf_op jit(solution)/shard_map/sub | solution.py:477
  54.3 0.0 copy-done.3
  54.3 0.0 copy-start.2
  54.3 1.1 %convert_element_type.6 = f32[128,2048]{1,0:T(8,128)} convert(bf16[128,2048]{1,0:T(8,128)(2,1)S(1)} %copy-done.3) | non-fusion elementwise | flops 262144 | bytes 1572864 | tf_op jit(solution)/shard_map/convert_element_type | solution.py:478
  55.4 0.1 copy-done.2
  55.4 0.0 copy-start.4
  55.4 1.1 %convert_element_type.7 = f32[128,2048]{1,0:T(8,128)} convert(bf16[128,2048]{1,0:T(8,128)(2,1)S(1)} %copy-done.2) | non-fusion elementwise | flops 262144 | bytes 1572864 | tf_op jit(solution)/shard_map/convert_element_type | solution.py:478
  56.5 0.0 copy-done.4
  56.5 0.7 %copy.17 = f32[256,128]{1,0:T(8,128)} copy(f32[256,128]{1,0:T(8,128)S(1)} %copy-done.4) | data formatting | bytes 262144
Async XLA Ops:
  0.6 0.7 %copy-start.5 = (bf16[2048]{0:T(1024)(128)(2,1)S(1)}, bf16[2048]{0:T(1024)(128)(2,1)}, u32[]{:S(2)}) copy-start(bf16[2048]{0:T(1024)(128)(2,1)} %param.21) | copy-start | bytes 12292
  1.9 49.8 %copy-start = (f32[1536,128]{1,0:T(8,128)S(1)}, f32[1536,128]{1,0:T(8,128)}, u32[]{:S(2)}) copy-start(f32[1536,128]{1,0:T(8,128)} %table_ref.1) | copy-start | bytes 2359300
  1.9 49.9 %copy-start.1 = (f32[1536,128]{1,0:T(8,128)S(1)}, f32[1536,128]{1,0:T(8,128)}, u32[]{:S(2)}) copy-start(f32[1536,128]{1,0:T(8,128)} %param.16) | copy-start | bytes 2359300
  51.8 2.5 %copy-start.3 = (bf16[128,2048]{1,0:T(8,128)(2,1)S(1)}, bf16[128,2048]{1,0:T(8,128)(2,1)}, u32[]{:S(2)}) copy-start(bf16[128,2048]{1,0:T(8,128)(2,1)} %get-tuple-element.10) | copy-start | bytes 1572868
  54.3 1.1 %copy-start.2 = (bf16[128,2048]{1,0:T(8,128)(2,1)S(1)}, bf16[128,2048]{1,0:T(8,128)(2,1)}, u32[]{:S(2)}) copy-start(bf16[128,2048]{1,0:T(8,128)(2,1)} %get-tuple-element.11) | copy-start | bytes 1572868
  55.4 1.1 %copy-start.4 = (f32[256,128]{1,0:T(8,128)S(1)}, f32[256,128]{1,0:T(8,128)}, u32[]{:S(2)}) copy-start(f32[256,128]{1,0:T(8,128)} %get-tuple-element.24) | copy-start | bytes 393220

commit v3 on v2

--- a/solution.py
+++ b/solution.py
@@ -33,12 +33,14 @@
     grads_ref,
     place_ref,
     table_ref,
+    accum_ref,
     labels_ref,
     gain_ref,
     wg_ref,
     wu_ref,
     wo_ref,
-    total_ref,
+    new_table_ref,
+    new_accum_ref,
     gate_ref,
     up_ref,
     emb_ref,
@@ -387,12 +389,15 @@
     tower.spread_z()
     tower.spread_x()
     sums.finish()
-    total_ref[...] = tall[...]
+    summed = tall[...]
+    squares = accum_ref[...] + summed * summed
+    new_accum_ref[...] = squares
+    new_table_ref[...] = table_ref[...] - learn_rate * summed * lax.rsqrt(squares)
     tower.finish()
     for b in range(hid // 128):
         cols = slice(b * 128, (b + 1) * 128)
-        gate_ref[:, cols] = gtotal[cols, :]
-        up_ref[:, cols] = gtotal[hid + b * 128 : hid + (b + 1) * 128, :]
+        gate_ref[:, cols] = gtotal[cols, :].astype(F32)
+        up_ref[:, cols] = gtotal[hid + b * 128 : hid + (b + 1) * 128, :].astype(F32)
     for one in pending:
         one.wait_send()
 
@@ -412,16 +417,17 @@
     vmem = pl.BlockSpec(memory_space=pltpu.VMEM)
     n_peer = max(n_emb - 1, 1)
     dma = pltpu.SemaphoreType.DMA
-    total, gate, up, emb_grad = pl.pallas_call(
+    return pl.pallas_call(
         functools.partial(tower_kernel, n_dp, n_emb, scale),
         out_shape=(
             jax.ShapeDtypeStruct((rows, width), F32),
-            jax.ShapeDtypeStruct((width, hid), BF16),
-            jax.ShapeDtypeStruct((width, hid), BF16),
+            jax.ShapeDtypeStruct((rows, width), F32),
+            jax.ShapeDtypeStruct((width, hid), F32),
+            jax.ShapeDtypeStruct((width, hid), F32),
             jax.ShapeDtypeStruct((tok, width), F32),
         ),
-        in_specs=[vmem] * 10,
-        out_specs=(vmem,) * 4,
+        in_specs=[vmem] * 11,
+        out_specs=(vmem,) * 5,
         scratch_shapes=[
             pltpu.VMEM((rows, width), BF16),
             pltpu.VMEM((n_emb, 8, 2 * tok), jnp.int32),
@@ -467,15 +473,13 @@
         prev_grads,
         row_place.reshape(1, -1),
         table,
+        accum,
         labels.reshape(1, -1),
         gain.reshape(1, -1),
         w_gate,
         w_up,
         w_out.reshape(1, -1),
     )
-    new_accum = accum + total * total
-    new_table = table - learn_rate * total * lax.rsqrt(new_accum)
-    return (new_table, new_accum, gate.astype(F32), up.astype(F32), emb_grad)
 
 
 def solution(mesh):

time: 57.4 us -> 59.7 us (1.040)
  local copies, waits for them, and re-layouts: 2.02 us -> 8.21 us
  other arithmetic: 4.62 us -> 0 us
  Pallas kernels: 49.8 us -> 50.5 us
    unnamed x13 -> x15, local copies, waits for them, and re-layouts: 1.41 us -> 7.61 us
    sub x1 -> x0, other arithmetic: 2.48 us -> none  [on_device(): new_table = table - learn_rate * total * lax.rsqrt(new_accum)]
    convert_element_type x2 -> x0, other arithmetic: 2.14 us -> none  [on_device(): return (new_table, new_accum, gate.astype(F32), up.astype(F32), emb_grad)]
    pallas_call x1, Pallas kernels: 49.8 us -> 50.5 us  [on_device(): pl.pallas_call(functools.partial(tower_kernel, n_dp, n_emb, scale), out_s...]
where the time goes in v3:
time: 59.7 us; the launch traced here: 59.4 us
  Pallas kernels  50.5 us (85%)
  local copies, waits for them, and re-layouts  8.21 us (14%)
  between operations  0.66 us (1%)
    pallas_call x1, Pallas kernels, on_device(): pl.pallas_call(functools.partial(tower_kernel, n_dp, n_emb, scale), out_s...  50.5 us
    unnamed x15, local copies, waits for them, and re-layouts  7.61 us

profile of v3, /device:TPU:1, one launch (start us, length us, event | category | flops | bytes accessed | tf_op | source)
XLA Modules:
  0.0 59.4 jit_solution(6968190003599721537)
XLA Ops:
  0.6 0.0 copy-start.4
  0.6 0.7 %copy-done.4 = bf16[2048]{0:T(1024)(128)(2,1)S(1)} copy-done((bf16[2048]{0:T(1024)(128)(2,1)S(1)}, bf16[2048]{0:T(1024)(128)(2,1)}, u32[]{:S(2)}) %copy-start.4) | copy-done | bytes 4120
  1.3 0.6 %reshape.33.wo_ref = bf16[1,2048]{1,0:T(2,128)(2,1)} reshape(bf16[2048]{0:T(1024)(128)(2,1)S(1)} %copy-done.4) | data formatting | bytes 8192 | tf_op jit(solution)/shard_map/reshape | solution.py:481
  1.9 50.5 %shard_map.146 = (f32[1536,128]{1,0:T(8,128)}, f32[1536,128]{1,0:T(8,128)}, f32[128,2048]{1,0:T(8,128)}, f32[128,2048]{1,0:T(8,128)}, f32[256,128]{1,0:T(8,128)}) custom-call(s32[1,256]{1,0:T(1,128)} %bitcast.7, s32[1,256]{1,0:T(1,128)} %bitcast.8, bf16[256,128]{1,0:T(8,128)(2,1)} %grads_ref.1, s32[1,3072]{1,0:T(1,128)} %bitcast.5, f32[1536,128]{1,0:T(8,128)} %table_ref.1, ...), custom_call_target="tpu_custom_call" | custom-call | tf_op jit(solution)/shard_map/pallas_call | solution.py:420
  52.5 0.0 copy-start.2
  52.5 2.1 %copy.21 = f32[1536,128]{1,0:T(8,128)} copy(f32[1536,128]{1,0:T(8,128)} %get-tuple-element.10) | data formatting | bytes 1572864
  54.6 0.0 copy-done.2
  54.6 0.0 copy-start.1
  54.6 0.9 %copy.22 = f32[1536,128]{1,0:T(8,128)} copy(f32[1536,128]{1,0:T(8,128)S(1)} %copy-done.2) | data formatting | bytes 1572864
  55.5 0.6 %copy-done.1 = f32[128,2048]{1,0:T(8,128)S(1)} copy-done((f32[128,2048]{1,0:T(8,128)S(1)}, f32[128,2048]{1,0:T(8,128)}, u32[]{:S(2)}) %copy-start.1) | copy-done | bytes 1048600
  56.1 0.0 copy-start
  56.1 1.0 %copy.23 = f32[128,2048]{1,0:T(8,128)} copy(f32[128,2048]{1,0:T(8,128)S(1)} %copy-done.1) | data formatting | bytes 2097152
  57.1 0.6 %copy-done = f32[128,2048]{1,0:T(8,128)S(1)} copy-done((f32[128,2048]{1,0:T(8,128)S(1)}, f32[128,2048]{1,0:T(8,128)}, u32[]{:S(2)}) %copy-start) | copy-done | bytes 1048600
  57.7 0.0 copy-start.3
  57.7 1.0 %copy.24 = f32[128,2048]{1,0:T(8,128)} copy(f32[128,2048]{1,0:T(8,128)S(1)} %copy-done) | data formatting | bytes 2097152
  58.7 0.1 copy-done.3
  58.8 0.7 %copy.25 = f32[256,128]{1,0:T(8,128)} copy(f32[256,128]{1,0:T(8,128)S(1)} %copy-done.3) | data formatting | bytes 262144
Async XLA Ops:
  0.6 0.7 %copy-start.4 = (bf16[2048]{0:T(1024)(128)(2,1)S(1)}, bf16[2048]{0:T(1024)(128)(2,1)}, u32[]{:S(2)}) copy-start(bf16[2048]{0:T(1024)(128)(2,1)} %param.21) | copy-start | bytes 12292
  52.5 2.1 %copy-start.2 = (f32[1536,128]{1,0:T(8,128)S(1)}, f32[1536,128]{1,0:T(8,128)}, u32[]{:S(2)}) copy-start(f32[1536,128]{1,0:T(8,128)} %get-tuple-element.11) | copy-start | bytes 2359300
  54.6 1.5 %copy-start.1 = (f32[128,2048]{1,0:T(8,128)S(1)}, f32[128,2048]{1,0:T(8,128)}, u32[]{:S(2)}) copy-start(f32[128,2048]{1,0:T(8,128)} %get-tuple-element.12) | copy-start | bytes 3145732
  56.1 1.6 %copy-start = (f32[128,2048]{1,0:T(8,128)S(1)}, f32[128,2048]{1,0:T(8,128)}, u32[]{:S(2)}) copy-start(f32[128,2048]{1,0:T(8,128)} %get-tuple-element.13) | copy-start | bytes 3145732
  57.7 1.0 %copy-start.3 = (f32[256,128]{1,0:T(8,128)S(1)}, f32[256,128]{1,0:T(8,128)}, u32[]{:S(2)}) copy-start(f32[256,128]{1,0:T(8,128)} %get-tuple-element.14) | copy-start | bytes 393220
